TPU v7x, 32 devices: a whole 2x2x4 slice. The times are simulated.
32 devices in a mesh: owner: 4 (over y, x), rows: 8 (over z, core).
Axes of the slice: x: 2, y: 2, z: 4, core: 2. Of those that a mesh axis runs over, the one named last changes fastest.
Arguments:
- train_gate: float32 [128, 2048, 768], P('owner', 'rows'), may hold values from -0.1875 to 0.1875
- other_gate: bfloat16 [128, 2048, 768], P('owner', 'rows'), may hold values from -0.0625 to 0.0625
- train_up: float32 [128, 2048, 768], P('owner', 'rows'), may hold values from -0.1875 to 0.1875
- other_up: bfloat16 [128, 2048, 768], P('owner', 'rows'), may hold values from -0.0625 to 0.0625
- router_weight: float32 [2048, 128], P('rows', 'owner'), may hold values from -0.125 to 0.125
- router_gain: float32 [2048], P('rows'), may hold values from 0.25 to 1.75
Outputs:
- ready_gate: bfloat16 [128, 2048, 768], P(('owner', 'rows'))
- ready_up: bfloat16 [128, 2048, 768], P(('owner', 'rows'))
- scale_gate: float32 [128, 768], P(('owner', 'rows'))
- scale_up: float32 [128, 768], P(('owner', 'rows'))
- serve_router: bfloat16 [2048, 128], replicated
All inputs are finite; a program needn't handle non-finite values. Where the computation divides by a largest or mean magnitude, that divisor is 1e-20 or more.
Results may differ from a plain program's by a relative error of at most 0.001.
Values may be sent and summed in bfloat16 or wider, within the bound.
A program may use at most 192 MiB of HBM per device.

v0:
```python
import functools

import jax
import jax.numpy as jnp
from jax import lax
from jax.experimental import pallas as pl
from jax.experimental.pallas import tpu as pltpu
from jax.sharding import PartitionSpec as P

F32, BF16 = jnp.float32, jnp.bfloat16
CHUNK = 32


def flipped(me, k, n):
    out, bit = 0, 1
    while bit < n:
        out = out + ((me // bit + k // bit) % 2) * bit
        bit *= 2
    return out


def kernel(n, owners, each, train_gate, other_gate, train_up, other_up, part_router,
           ready_gate, ready_up, scales, router,
           wide, narrow, send, mxs, rxs, fulls, totals,
           load_sem, send_sem, recv_sem, own_sem, mx_sem, rx_sem, fl_sem, fr_sem,
           rt_send, rt_recv, ro_send, ro_recv, rt_own):
    me, owner = lax.axis_index("rows"), lax.axis_index("owner")
    rows = wide.shape[2]
    units = 2 * each
    trains, others, readies = (train_gate, train_up), (other_gate, other_up), (ready_gate, ready_up)

    first = mxs[0].shape[1]
    batches = (range(first), range(first, units))
    order = ([(0, u) for u in batches[0]] + [(1, 0)] + [(0, u) for u in batches[1]]
             + [(1, u) for u in range(1, units)])

    def loads(step):
        unit, slot = order[step][1], step % 2
        kind, j = unit // each, unit % each
        return (
            pltpu.make_async_copy(trains[kind].at[:, j], wide.at[slot], load_sem.at[slot, 0]),
            pltpu.make_async_copy(others[kind].at[:, j], narrow.at[slot], load_sem.at[slot, 1]),
        )

    def start(step):
        if step < len(order):
            for copy in loads(step):
                copy.start()

    def remote(src, dst, s, r, **where):
        return pltpu.make_async_remote_copy(
            src_ref=src, dst_ref=dst, send_sem=s, recv_sem=r, device_id=where,
            device_id_type=pl.DeviceIdType.MESH,
        )

    start(0)
    start(1)
    barrier = pltpu.get_barrier_semaphore()
    for k in range(1, n):
        pl.semaphore_signal(barrier, inc=1, device_id={"rows": (me + k) % n},
                            device_id_type=pl.DeviceIdType.MESH)
    for k in range(1, owners):
        pl.semaphore_signal(barrier, inc=1, device_id={"owner": (owner + k) % owners},
                            device_id_type=pl.DeviceIdType.MESH)
    pl.semaphore_wait(barrier, n - 1 + owners - 1)

    def router_rows(k):
        return remote(part_router, router.at[owner, me], rt_send.at[k], rt_recv.at[k],
                      rows=(me + k) % n)

    def router_owners(k):
        return remote(router.at[owner], router.at[owner], ro_send.at[k], ro_recv.at[k],
                      owner=(owner + k) % owners)

    own_router = pltpu.make_async_copy(part_router, router.at[owner, me], rt_own)
    own_router.start()
    for k in range(1, n):
        router_rows(k).start()

    def maxima(b, unit):
        step = order.index((0, unit))
        slot, row = step % 2, unit - batches[b][0]
        for copy in loads(step):
            copy.wait()

        def largest(d, _):
            acc = None
            for i in range(rows // CHUNK):
                x = wide[slot, d, i * CHUNK:(i + 1) * CHUNK, :]
                y = narrow[slot, d, i * CHUNK:(i + 1) * CHUNK, :].astype(F32)
                a = jnp.abs(x + y)
                acc = a if acc is None else jnp.maximum(acc, a)
            mxs[b][d, row:row + 1, :] = jnp.max(acc, axis=0, keepdims=True)
            return 0

        lax.fori_loop(0, n, largest, 0)
        start(step + 2)

    def to_owner(b, k):
        d = (me + k) % n
        return remote(mxs[b].at[d], rxs[b].at[me], mx_sem.at[b, k], rx_sem.at[b, k], rows=d)

    def to_all(b, k):
        return remote(totals[b], fulls[b].at[me], fl_sem.at[b, k], fr_sem.at[b, k],
                      rows=(me + k) % n)

    def give(b):
        for k in range(1, n):
            to_owner(b, k).start()
        rxs[b][me] = mxs[b][me]

    def combine(b):
        for k in range(1, n):
            to_owner(b, k).wait()
        total = rxs[b][0]
        for d in range(1, n):
            total = jnp.maximum(total, rxs[b][d])
        totals[b][...] = total
        fulls[b][me] = total
        for k in range(1, n):
            to_all(b, k).start()
        for at, unit in enumerate(batches[b]):
            scales[unit:unit + 1, :] = total[at:at + 1, :]

    def gathered(b):
        for k in range(1, n):
            to_all(b, k).wait()

    far, near = list(range(n // 2, n)), list(range(2, n // 2))
    side = me % 2

    def dest(p):
        a, b, c = len(far), len(near), n // 2
        in_far = jnp.where(side == 0, p < a, jnp.logical_and(p >= b, p < a + b))
        at_far = p - side * b
        at_near = p - (1 - side) * a
        k = jnp.where(p == n - 2, 1, jnp.where(in_far, c + at_far, 2 + at_near))
        return flipped(me, k, n)

    def data(unit, p, d):
        kind, j = unit // each, unit % each
        return remote(send.at[unit, p], readies[kind].at[j, me], send_sem.at[unit, p],
                      recv_sem.at[unit, me], rows=d)

    def own(unit):
        kind, j = unit // each, unit % each
        return pltpu.make_async_copy(send.at[unit, n - 1], readies[kind].at[j, me], own_sem.at[unit])

    def blocks(unit):
        step = order.index((1, unit))
        slot, b = step % 2, 0 if unit < first else 1
        row = unit - batches[b][0]
        for copy in loads(step):
            copy.wait()

        def scaled(p, d):
            inverse = 1.0 / fulls[b][d, row:row + 1, :]
            for i in range(rows // CHUNK):
                x = wide[slot, d, i * CHUNK:(i + 1) * CHUNK, :]
                y = narrow[slot, d, i * CHUNK:(i + 1) * CHUNK, :].astype(F32)
                send[unit, p, i * CHUNK:(i + 1) * CHUNK, :] = ((x + y) * inverse).astype(BF16)

        def one(p, _):
            d = dest(p)
            scaled(p, d)
            data(unit, p, d).start()
            return 0

        lax.fori_loop(0, n - 1, one, 0)
        scaled(n - 1, me)
        own(unit).start()
        start(step + 2)

    for unit in batches[0]:
        maxima(0, unit)
    give(0)
    combine(0)
    gathered(0)
    blocks(0)
    for unit in batches[1]:
        maxima(1, unit)
    give(1)
    own_router.wait()
    for k in range(1, n):
        router_rows(k).wait()
    for k in range(1, owners):
        router_owners(k).start()
    middle = max(first - 1, 1)
    for unit in range(1, middle):
        blocks(unit)
    combine(1)
    for unit in range(middle, first):
        blocks(unit)
    gathered(1)
    for unit in batches[1]:
        blocks(unit)

    for unit in range(units):
        kind, j = unit // each, unit % each

        def ended(k, _, unit=unit, kind=kind, j=j):
            d = (me + k) % n
            remote(send.at[unit, k - 1], readies[kind].at[j, d], send_sem.at[unit, k - 1],
                   recv_sem.at[unit, d], rows=d).wait()
            return 0

        lax.fori_loop(1, n, ended, 0)
        own(unit).wait()
    for k in range(1, owners):
        router_owners(k).wait()


def per_device(n, owners, train_gate, other_gate, train_up, other_up, router_weight, router_gain):
    experts, rows, width = train_gate.shape
    each = experts // n
    units = 2 * each
    first = max(1, 3 * units // 8)
    sizes = (first, units - first)
    columns = router_weight.shape[1]
    part = (router_weight * router_gain[:, None]).astype(BF16)
    lanes = 128 if rows * columns % (128 * 16) == 0 else columns
    part = part.reshape(rows * columns // lanes, lanes)
    blocks = [x.reshape(n, each, rows, width) for x in (train_gate, other_gate, train_up, other_up)]
    hbm, vmem = pl.BlockSpec(memory_space=pl.ANY), pl.BlockSpec(memory_space=pltpu.VMEM)
    ready = jax.ShapeDtypeStruct((each, n, rows, width), BF16)
    dma = pltpu.SemaphoreType.DMA
    ready_gate, ready_up, scales, router = pl.pallas_call(
        functools.partial(kernel, n, owners, each),
        out_shape=(
            ready, ready,
            jax.ShapeDtypeStruct((units, width), F32),
            jax.ShapeDtypeStruct((owners, n) + part.shape, BF16),
        ),
        in_specs=[hbm] * 4 + [vmem],
        out_specs=(hbm, hbm, vmem, hbm),
        scratch_shapes=[
            pltpu.VMEM((2, n, rows, width), F32),
            pltpu.VMEM((2, n, rows, width), BF16),
            pltpu.VMEM((units, n, rows, width), BF16),
            [pltpu.VMEM((n, size, width), F32) for size in sizes],
            [pltpu.VMEM((n, size, width), F32) for size in sizes],
            [pltpu.VMEM((n, size, width), F32) for size in sizes],
            [pltpu.VMEM((size, width), F32) for size in sizes],
            dma((2, 2)), dma((units, n)), dma((units, n)), dma((units,)),
            dma((2, n)), dma((2, n)), dma((2, n)), dma((2, n)),
            dma((n,)), dma((n,)), dma((owners,)), dma((owners,)), dma(()),
        ],
        compiler_params=pltpu.CompilerParams(
            collective_id=0, has_side_effects=True, vmem_limit_bytes=60 * 1024 * 1024
        ),
    )(*blocks, part)
    ready_gate, ready_up = (x.reshape(each, n * rows, width) for x in (ready_gate, ready_up))
    serve_router = (
        router.reshape(owners, n * rows, columns).transpose(1, 0, 2).reshape(n * rows, owners * columns)
    )
    return (ready_gate, ready_up, scales[:each], scales[each:], serve_router)


def solution(mesh):
    n, owners = mesh.shape["rows"], mesh.shape["owner"]
    in_specs = (
        P("owner", "rows", None),
        P("owner", "rows", None),
        P("owner", "rows", None),
        P("owner", "rows", None),
        P("rows", "owner"),
        P("rows"),
    )
    out_specs = (
        P(("owner", "rows"), None, None),
        P(("owner", "rows"), None, None),
        P(("owner", "rows"), None),
        P(("owner", "rows"), None),
        P(),
    )
    return jax.shard_map(
        functools.partial(per_device, n, owners), mesh=mesh, in_specs=in_specs,
        out_specs=out_specs, check_vma=False,
    )
```

profile of v0, /device:TPU:11, one launch (start us, length us, event | category | flops | bytes accessed | tf_op | source)
XLA Modules:
  0.0 601.2 jit_solution(14819152855040770210)
XLA Ops:
  0.6 0.8 multiply_convert_fusion
  1.4 0.1 copy.13
  1.5 0.7 reshape.42.part_router
  2.2 572.2 %shard_map.101 = (bf16[4,8,256,768]{3,2,1,0:T(8,128)(2,1)}, bf16[4,8,256,768]{3,2,1,0:T(8,128)(2,1)}, f32[8,768]{1,0:T(8,128)}, bf16[4,8,64,128]{3,2,1,0:T(8,128)(2,1)}) custom-call(f32[8,4,256,768]{3,2,1,0:T(8,128)} %bitcast.10, bf16[8,4,256,768]{3,2,1,0:T(8,128)(2,1)} %bitcast.12, f32[8,4,256,768]{3,2,1,0:T(8,128)} %bitcast.11, ...), custom_call_target="tpu_custom_call" | custom-call | tf_op jit(solution)/shard_map/pallas_call | solution.py:227
  574.4 1.4 fusion
  575.8 2.6 reshape.45
  578.5 0.8 copy.14
  579.3 1.0 copy.15
  580.3 10.4 %copy.18 = bf16[4,2048,768]{2,1,0:T(8,128)(2,1)} copy(bf16[4,2048,768]{2,1,0:T(8,128)(2,1)} %bitcast.15) | data formatting | bytes 25165824
  590.8 10.4 %copy.19 = bf16[4,2048,768]{2,1,0:T(8,128)(2,1)} copy(bf16[4,2048,768]{2,1,0:T(8,128)(2,1)} %bitcast.14) | data formatting | bytes 25165824
where the time goes:
time: 602 us; the launch traced here: 601 us
  Pallas kernels  572 us (95%)
  local copies, waits for them, and re-layouts  27.6 us (5%)
    pallas_call x1, Pallas kernels, per_device(): pl.pallas_call(functools.partial(kernel, n, owners, each), out_shape=(rea...  572 us
    unnamed x3, local copies, waits for them, and re-layouts  21.9 us

commit v1 on v0

v1 whole, which is shorter than its diff:
```python
import functools

import jax
import jax.numpy as jnp
from jax import lax
from jax.experimental import pallas as pl
from jax.experimental.pallas import tpu as pltpu
from jax.sharding import PartitionSpec as P

F32, BF16 = jnp.float32, jnp.bfloat16
CHUNK = 32
AHEAD = 4


def flipped(me, k, n):
    out, bit = 0, 1
    while bit < n:
        out = out + ((me // bit + k // bit) % 2) * bit
        bit *= 2
    return out


def kernel(n, owners, each, train_gate, other_gate, train_up, other_up, part_router,
           ready_gate, ready_up, scale_gate, scale_up, router,
           wide, narrow, send, maxes, gathered, halves, mirrored, full, padded, pieces,
           load_sem, send_sem, recv_sem,
           as_sem, ar_sem, bs_sem, br_sem, cs_sem, cr_sem,
           r1_send, r1_recv, r2_send, r2_recv, r3_send, r3_recv, r4_send, r4_recv, r5_send, r5_recv):
    me, owner = lax.axis_index("rows"), lax.axis_index("owner")
    rows = wide.shape[2]
    units = 2 * each
    half = n // 2
    spot = me % half
    base = me - spot
    mirror = (me + half) % n
    slots = send.shape[0]
    trains, others, readies = (train_gate, train_up), (other_gate, other_up), (ready_gate, ready_up)
    scales = (scale_gate, scale_up)

    def remote(src, dst, s, r, **where):
        return pltpu.make_async_remote_copy(
            src_ref=src, dst_ref=dst, send_sem=s, recv_sem=r, device_id=where,
            device_id_type=pl.DeviceIdType.MESH,
        )

    def loads(unit, d):
        kind, j, slot = unit // each, unit % each, unit % 2
        return (
            pltpu.make_async_copy(trains[kind].at[d, j], wide.at[slot, d], load_sem.at[slot, d, 0]),
            pltpu.make_async_copy(others[kind].at[d, j], narrow.at[slot, d], load_sem.at[slot, d, 1]),
        )

    def pair(k):
        return (spot + k) % half

    def start(unit):
        if unit < units:
            def one(k, _):
                for s in range(2):
                    for copy in loads(unit, 2 * pair(k) + s):
                        copy.start()
                return 0

            lax.fori_loop(1, half + 1, one, 0)

    start(0)
    barrier = pltpu.get_barrier_semaphore()
    for k in range(1, n):
        pl.semaphore_signal(barrier, inc=1, device_id={"rows": (me + k) % n},
                            device_id_type=pl.DeviceIdType.MESH)
    for k in range(1, owners):
        pl.semaphore_signal(barrier, inc=1, device_id={"owner": (owner + k) % owners},
                            device_id_type=pl.DeviceIdType.MESH)
    pl.semaphore_wait(barrier, n - 1 + owners - 1)

    def to_spot(unit, k):
        q = pair(k)
        return remote(maxes.at[unit, q], gathered.at[unit, spot], as_sem.at[unit, k],
                      ar_sem.at[unit, k], rows=base + q)

    def to_mirror(unit):
        return remote(halves.at[unit], mirrored.at[unit], bs_sem.at[unit], br_sem.at[unit], rows=mirror)

    def to_half(unit, k):
        return remote(full.at[unit, spot], full.at[unit, spot], cs_sem.at[unit, k],
                      cr_sem.at[unit, k], rows=base + pair(k))

    def maxima(unit):
        slot = unit % 2

        def largest(d):
            acc = None
            for i in range(rows // CHUNK):
                x = wide[slot, d, i * CHUNK:(i + 1) * CHUNK, :]
                y = narrow[slot, d, i * CHUNK:(i + 1) * CHUNK, :].astype(F32)
                a = jnp.abs(x + y)
                acc = a if acc is None else jnp.maximum(acc, a)
            return jnp.max(acc, axis=0, keepdims=True)

        def both(k, _):
            q = pair(k)
            for s in range(2):
                for copy in loads(unit, 2 * q + s):
                    copy.wait()
                maxes[unit, q, s:s + 1, :] = largest(2 * q + s)
            return 0

        def shared(k, _):
            both(k, 0)
            to_spot(unit, k).start()
            return 0

        lax.fori_loop(1, half, shared, 0)
        both(0, 0)
        gathered[unit, spot] = maxes[unit, spot]

    def exchange(unit):
        kind, j = unit // each, unit % each
        for k in range(1, half):
            to_spot(unit, k).wait()
        mine = gathered[unit, 0]
        for q in range(1, half):
            mine = jnp.maximum(mine, gathered[unit, q])
        halves[unit] = mine
        to_mirror(unit).start()
        to_mirror(unit).wait()
        full[unit, spot] = jnp.maximum(mine, mirrored[unit])
        for k in range(1, half):
            to_half(unit, k).start()
        for k in range(1, half):
            to_half(unit, k).wait()
        scales[kind][j:j + 1, :] = scale_of(unit, me)

    def scale_of(unit, d):
        two = full[unit, d // 2]
        return jnp.where(d % 2 == 0, two[0:1], two[1:2])

    far, near = list(range(n // 2, n)), list(range(2, n // 2))
    side = me % 2

    def dest(p):
        a, b, c = len(far), len(near), n // 2
        in_far = jnp.where(side == 0, p < a, jnp.logical_and(p >= b, p < a + b))
        at_far = p - side * b
        at_near = p - (1 - side) * a
        k = jnp.where(p == n - 2, 1, jnp.where(in_far, c + at_far, 2 + at_near))
        return flipped(me, k, n)

    def data(unit, p, d):
        kind, j, slot = unit // each, unit % each, unit % slots
        return remote(send.at[slot, p], readies[kind].at[j, me], send_sem.at[slot, p],
                      recv_sem.at[unit, me], rows=d)

    def blocks(unit):
        slot = unit % 2
        kind, j = unit // each, unit % each

        def scaled(d, put):
            inverse = 1.0 / scale_of(unit, d)
            for i in range(rows // CHUNK):
                x = wide[slot, d, i * CHUNK:(i + 1) * CHUNK, :]
                y = narrow[slot, d, i * CHUNK:(i + 1) * CHUNK, :].astype(F32)
                put(slice(i * CHUNK, (i + 1) * CHUNK), ((x + y) * inverse).astype(BF16))

        def one(p, _):
            d = dest(p)
            if unit >= slots:
                data(unit - slots, p, d).wait_send()

            def put(at, value):
                send[unit % slots, p, at, :] = value

            scaled(d, put)
            data(unit, p, d).start()
            return 0

        lax.fori_loop(0, n - 1, one, 0)

        def put(at, value):
            readies[kind][j, me, at, :] = value

        scaled(me, put)

    rows_of = rows // owners

    def block_of(r):
        return pl.ds(pl.multiple_of(r * rows, rows), rows)

    def share_of(r, o):
        return pl.ds(pl.multiple_of(r * rows + o * rows_of, rows_of), rows_of)

    def r1(k):
        return remote(padded, pieces.at[owner], r1_send.at[k], r1_recv.at[k], owner=(owner + k) % owners)

    def r2(k):
        at = router.at[block_of(me)]
        return remote(at, at, r2_send.at[k], r2_recv.at[k], rows=base + pair(k))

    def r3():
        at = router.at[share_of(me, owner)]
        return remote(at, at, r3_send, r3_recv, rows=mirror)

    def r4(k):
        at = router.at[share_of(mirror, owner)]
        return remote(at, at, r4_send.at[k], r4_recv.at[k], owner=(owner + k) % owners)

    def r5(k):
        at = router.at[block_of(mirror)]
        return remote(at, at, r5_send.at[k], r5_recv.at[k], rows=base + pair(k))

    def router_owners():
        columns, lanes = part_router.shape[1], padded.shape[1]
        lane = lax.broadcasted_iota(jnp.int32, (columns, lanes), 1)
        row = lax.broadcasted_iota(jnp.int32, (columns, lanes), 0)
        place = (lane == row + owner * columns).astype(F32).astype(BF16)
        padded[...] = jnp.dot(part_router[...], place, preferred_element_type=F32).astype(BF16)
        pieces[owner] = padded[...]
        for k in range(1, owners):
            r1(k).start()

    def router_rows():
        for k in range(1, owners):
            r1(k).wait()
        total = pieces[0].astype(F32)
        for o in range(1, owners):
            total = total + pieces[o].astype(F32)
        router[block_of(me), :] = total.astype(BF16)
        r3().start()
        for k in range(1, half):
            r2(k).start()

    def router_across():
        r3().wait()
        for k in range(1, owners):
            r4(k).start()

    def router_far():
        for k in range(1, owners):
            r4(k).wait()
        for k in range(1, half):
            r5(k).start()

    stages = [router_owners, router_rows, router_across, router_far]
    for unit in range(units):
        maxima(unit)
        start(unit + 1)
        exchange(unit)
        blocks(unit)
        if stages:
            stages.pop(0)()
    for stage in stages:
        stage()
    for k in range(1, half):
        r2(k).wait()
        r5(k).wait()

    for unit in range(units):
        kind, j = unit // each, unit % each

        def ended(k, _, unit=unit, kind=kind, j=j):
            d = (me + k) % n
            copy = remote(send.at[unit % slots, k - 1], readies[kind].at[j, d],
                          send_sem.at[unit % slots, k - 1], recv_sem.at[unit, d], rows=d)
            if unit >= units - slots:
                copy.wait_send()
            copy.wait_recv()
            return 0

        lax.fori_loop(1, n, ended, 0)


def store(count, *refs):
    sources, results, sem = refs[:count], refs[count:2 * count], refs[2 * count]
    copies = []
    for i, (source, result) in enumerate(zip(sources, results)):
        copies.append(pltpu.make_async_copy(source, result, sem.at[i]))
    for copy in copies:
        copy.start()
    for copy in copies:
        copy.wait()


def stored(arrays):
    count = len(arrays)
    return pl.pallas_call(
        functools.partial(store, count),
        out_shape=tuple(jax.ShapeDtypeStruct(x.shape, x.dtype) for x in arrays),
        in_specs=[pl.BlockSpec(memory_space=pltpu.VMEM)] * count,
        out_specs=(pl.BlockSpec(memory_space=pl.ANY),) * count,
        scratch_shapes=[pltpu.SemaphoreType.DMA((count,))],
        compiler_params=pltpu.CompilerParams(vmem_limit_bytes=1024 * 1024),
    )(*arrays)


def per_device(n, owners, train_gate, other_gate, train_up, other_up, router_weight, router_gain):
    experts, rows, width = train_gate.shape
    each = experts // n
    units = 2 * each
    half = n // 2
    slots = min(units, AHEAD)
    columns = router_weight.shape[1]
    part = (router_weight * router_gain[:, None]).astype(BF16)
    blocks = [x.reshape(n, each, rows, width) for x in (train_gate, other_gate, train_up, other_up)]
    hbm, vmem = pl.BlockSpec(memory_space=pl.ANY), pl.BlockSpec(memory_space=pltpu.VMEM)
    dma = pltpu.SemaphoreType.DMA
    scratch = n * rows * width * (2 * 6 + slots * 2) + 4 * units * (3 * half + 2) * 2 * width * 4
    results = pl.pallas_call(
        functools.partial(kernel, n, owners, each),
        out_shape=(
            pltpu.VMEM((each, n, rows, width), BF16),
            pltpu.VMEM((each, n, rows, width), BF16),
            pltpu.VMEM((each, width), F32),
            pltpu.VMEM((each, width), F32),
            pltpu.VMEM((n * rows, owners * columns), BF16),
        ),
        in_specs=[hbm] * 4 + [vmem],
        out_specs=(vmem,) * 5,
        scratch_shapes=[
            pltpu.VMEM((2, n, rows, width), F32),
            pltpu.VMEM((2, n, rows, width), BF16),
            pltpu.VMEM((slots, n - 1, rows, width), BF16),
            pltpu.VMEM((units, half, 2, width), F32),
            pltpu.VMEM((units, half, 2, width), F32),
            pltpu.VMEM((units, 2, width), F32),
            pltpu.VMEM((units, 2, width), F32),
            pltpu.VMEM((units, half, 2, width), F32),
            pltpu.VMEM((rows, owners * columns), BF16),
            pltpu.VMEM((owners, rows, owners * columns), BF16),
            dma((2, n, 2)), dma((slots, n)), dma((units, n)),
            dma((units, half)), dma((units, half)), dma((units,)), dma((units,)),
            dma((units, half)), dma((units, half)),
            dma((owners,)), dma((owners,)), dma((half,)), dma((half,)), dma(()), dma(()),
            dma((owners,)), dma((owners,)), dma((half,)), dma((half,)),
        ],
        compiler_params=pltpu.CompilerParams(
            collective_id=0, has_side_effects=True, vmem_limit_bytes=scratch + 2 * 1024 * 1024
        ),
    )(*blocks, part)
    ready_gate, ready_up, scale_gate, scale_up, router = stored(results)
    ready_gate, ready_up = (x.reshape(each, n * rows, width) for x in (ready_gate, ready_up))
    return (ready_gate, ready_up, scale_gate, scale_up, router)


def solution(mesh):
    n, owners = mesh.shape["rows"], mesh.shape["owner"]
    in_specs = (
        P("owner", "rows", None),
        P("owner", "rows", None),
        P("owner", "rows", None),
        P("owner", "rows", None),
        P("rows", "owner"),
        P("rows"),
    )
    out_specs = (
        P(("owner", "rows"), None, None),
        P(("owner", "rows"), None, None),
        P(("owner", "rows"), None),
        P(("owner", "rows"), None),
        P(),
    )
    return jax.shard_map(
        functools.partial(per_device, n, owners), mesh=mesh, in_specs=in_specs,
        out_specs=out_specs, check_vma=False,
    )
```

time: 602 us -> 609 us (1.012)
  Pallas kernels: 572 us -> 605 us
  local copies, waits for them, and re-layouts: 27.6 us -> 0.85 us
    pallas_call x1 -> x2, Pallas kernels: 572 us -> 605 us  [the longest x1 597 us: per_device(): pl.pallas_call(functools.partial(kernel, n, owners, each), out_shape=(plt...]
    unnamed x3 -> x1, local copies, waits for them, and re-layouts: 21.9 us -> 0.85 us
where the time goes in v1:
time: 609 us; the launch traced here: 608 us
  Pallas kernels  605 us (99%)
    pallas_call x1, Pallas kernels, per_device(): pl.pallas_call(functools.partial(kernel, n, owners, each), out_shape=(plt...  597 us

profile of v1, /device:TPU:11, one launch (start us, length us, event | category | flops | bytes accessed | tf_op | source)
XLA Modules:
  0.0 608.4 jit_solution(17407518775956808646)
XLA Ops:
  0.6 0.9 copy.12
  1.5 1.4 multiply_convert_fusion.part_router
  2.9 596.5 %shard_map.101 = (bf16[4,8,256,768]{3,2,1,0:T(8,128)(2,1)S(1)}, bf16[4,8,256,768]{3,2,1,0:T(8,128)(2,1)S(1)}, f32[4,768]{1,0:T(4,128)S(1)}, f32[4,768]{1,0:T(4,128)S(1)}, bf16[2048,128]{1,0:T(8,128)(2,1)S(1)}) custom-call(f32[8,4,256,768]{3,2,1,0:T(8,128)} %bitcast.6, bf16[8,4,256,768]{3,2,1,0:T(8,128)(2,1)} %bitcast.8, f32[8,4,256,768]{3,2,1,0:T(8,128)} %bitcast.7, ...), custom_call_target="tpu_custom_call" | custom-call | tf_op jit(solution)/shard_map/pallas_call | solution.py:307
  599.4 9.0 %shard_map.102 = (bf16[4,8,256,768]{3,2,1,0:T(8,128)(2,1)}, bf16[4,8,256,768]{3,2,1,0:T(8,128)(2,1)}, f32[4,768]{1,0:T(4,128)}, f32[4,768]{1,0:T(4,128)}, bf16[2048,128]{1,0:T(8,128)(2,1)}) custom-call(bf16[4,8,256,768]{3,2,1,0:T(8,128)(2,1)S(1)} %get-tuple-element.15.refs_0_, bf16[4,8,256,768]{3,2,1,0:T(8,128)(2,1)S(1)} %get-tuple-element.16.refs_1_, ...), custom_call_target="tpu_custom_call" | custom-call | tf_op jit(solution)/shard_map/pallas_call | solution.py:285

commit v2 on v1

v2 whole, which is shorter than its diff:
```python
import functools

import jax
import jax.numpy as jnp
from jax import lax
from jax.experimental import pallas as pl
from jax.experimental.pallas import tpu as pltpu
from jax.sharding import PartitionSpec as P

F32, BF16 = jnp.float32, jnp.bfloat16
CHUNK = 32
PARTS, FAR_DEEP, NEAR_DEEP, SPLIT = 4, 3, 4, 2


def flipped(me, k, n):
    out, bit = 0, 1
    while bit < n:
        out = out + ((me // bit + k // bit) % 2) * bit
        bit *= 2
    return out


def kernel(n, owners, each, train_gate, other_gate, train_up, other_up, router_weight, router_gain,
           ready_gate, ready_up, scale_gate, scale_up, router,
           wide, narrow, send, maxes, gathered, halves, mirrored, full, solo, direct,
           weight, gain, padded, pieces,
           load_sem, send_sem, recv_sem, ds_sem, dr_sem, router_sem,
           as_sem, ar_sem, bs_sem, br_sem, cs_sem, cr_sem,
           r1_send, r1_recv, r2_send, r2_recv, r3_send, r3_recv, r4_send, r4_recv, r5_send, r5_recv):
    me, owner = lax.axis_index("rows"), lax.axis_index("owner")
    rows = wide.shape[2]
    units = 2 * each
    half = n // 2
    spot = me % half
    base = me - spot
    mirror = (me + half) % n
    deep = send.shape[0]
    part = send.shape[1]
    parts = rows // part
    trains, others, readies = (train_gate, train_up), (other_gate, other_up), (ready_gate, ready_up)
    scales = (scale_gate, scale_up)

    def remote(src, dst, s, r, **where):
        return pltpu.make_async_remote_copy(
            src_ref=src, dst_ref=dst, send_sem=s, recv_sem=r, device_id=where,
            device_id_type=pl.DeviceIdType.MESH,
        )

    def loads(unit, q):
        kind, j, slot = unit // each, unit % each, unit % 2
        two = pl.ds(2 * q, 2)
        return (
            pltpu.make_async_copy(trains[kind].at[two, j], wide.at[slot, two], load_sem.at[slot, q, 0]),
            pltpu.make_async_copy(others[kind].at[two, j], narrow.at[slot, two], load_sem.at[slot, q, 1]),
        )

    def pair(k):
        return (spot + k) % half

    def start(unit):
        if unit < units:
            def one(k, _):
                for copy in loads(unit, pair(k)):
                    copy.start()
                return 0

            lax.fori_loop(1, half + 1, one, 0)

    start(0)
    barrier = pltpu.get_barrier_semaphore()
    for k in range(1, n):
        pl.semaphore_signal(barrier, inc=1, device_id={"rows": (me + k) % n},
                            device_id_type=pl.DeviceIdType.MESH)
    for k in range(1, owners):
        pl.semaphore_signal(barrier, inc=1, device_id={"owner": (owner + k) % owners},
                            device_id_type=pl.DeviceIdType.MESH)
    routing = (pltpu.make_async_copy(router_weight, weight, router_sem.at[0]),
               pltpu.make_async_copy(router_gain, gain, router_sem.at[1]))
    for copy in routing:
        copy.start()

    def to_spot(unit, k):
        q = pair(k)
        return remote(maxes.at[unit, q], gathered.at[unit, spot], as_sem.at[k],
                      ar_sem.at[k], rows=base + q)

    def to_mirror(unit):
        return remote(halves.at[unit], mirrored.at[unit], bs_sem.at[unit % 2], br_sem.at[unit % 2], rows=mirror)

    def to_half(unit, k):
        return remote(full.at[unit, spot], full.at[unit, spot], cs_sem.at[k],
                      cr_sem.at[k], rows=base + pair(k))

    def maxima(unit):
        slot = unit % 2

        def largest(d):
            acc = None
            for i in range(rows // CHUNK):
                x = wide[slot, d, i * CHUNK:(i + 1) * CHUNK, :]
                y = narrow[slot, d, i * CHUNK:(i + 1) * CHUNK, :].astype(F32)
                a = jnp.abs(x + y)
                acc = a if acc is None else jnp.maximum(acc, a)
            return jnp.max(acc, axis=0, keepdims=True)

        def both(k, _):
            q = pair(k)
            for copy in loads(unit, q):
                copy.wait()
            for s in range(2):
                d = 2 * q + s
                most = largest(d)
                maxes[unit, q, s:s + 1, :] = most
                if unit == 0:
                    solo[d] = most
            return 0

        def shared(k, _):
            both(k, 0)
            if unit > 0:
                to_spot(unit, k).start()
            return 0

        lax.fori_loop(1, half, shared, 0)
        both(0, 0)
        gathered[unit, spot] = maxes[unit, spot]
        if unit == 0:
            direct[me] = solo[mirror]

    def to_direct(k):
        r = (me + k) % n
        return remote(solo.at[(r + half) % n], direct.at[me], ds_sem.at[k], dr_sem.at[k], rows=r)

    def first_scale():
        for k in range(1, n):
            to_direct(k).wait()
        total = direct[0]
        for d in range(1, n):
            total = jnp.maximum(total, direct[d])
        return total

    def across(unit):
        for k in range(1, half):
            to_spot(unit, k).wait()
        mine = gathered[unit, 0]
        for q in range(1, half):
            mine = jnp.maximum(mine, gathered[unit, q])
        halves[unit] = mine
        to_mirror(unit).start()

    def spread(unit):
        to_mirror(unit).wait()
        full[unit, spot] = jnp.maximum(halves[unit], mirrored[unit])
        for k in range(1, half):
            to_half(unit, k).start()

    def known(unit):
        kind, j = unit // each, unit % each
        for k in range(1, half):
            to_half(unit, k).wait()
        scales[kind][j:j + 1, :] = scale_of(unit, me)

    def scale_of(unit, d):
        two = full[unit, d // 2]
        return jnp.where(d % 2 == 0, two[0:1], two[1:2])

    far_items, near_items = half * parts, (half - 2) * parts
    items = far_items + near_items + parts
    side = me % 2

    def item(unit, t):
        lead = parts if unit == 0 else 0
        mixed = far_items - lead + near_items
        after = jnp.maximum(t - lead, 0)
        phase = side * (2 * mixed // 3)
        near_at = (after * near_items + phase) // mixed
        leading, beside = t < lead, t >= lead + mixed
        is_far = jnp.logical_or(leading, jnp.logical_and(
            jnp.logical_not(beside), ((after + 1) * near_items + phase) // mixed == near_at))
        far_at = jnp.where(leading, t, lead + after - near_at)
        near_at = jnp.where(beside, near_items + t - lead - mixed, near_at)
        at = jnp.where(is_far, far_at, near_at)
        near_k = jnp.where(beside, 1, 2 + at // parts)
        d = flipped(me, jnp.where(is_far, half + at // parts, near_k), n)
        slot = jnp.where(is_far, (unit * far_items + far_at) % FAR_DEEP,
                         FAR_DEEP + (unit * (near_items + parts) + near_at) % NEAR_DEEP)
        fresh = at < jnp.where(is_far, FAR_DEEP, NEAR_DEEP)
        return d, at % parts, slot, fresh

    def part_of(piece):
        return pl.ds(pl.multiple_of(piece * part, part), part)

    def data(unit, d, piece, slot):
        kind, j = unit // each, unit % each
        return remote(send.at[slot], readies[kind].at[j, me, part_of(piece)], send_sem.at[slot],
                      recv_sem.at[kind, me], rows=d)

    def scaled(unit, d, piece, put, scale=None):
        inverse = 1.0 / (scale_of(unit, d) if scale is None else scale)
        chunk = min(CHUNK, part)
        for i in range(part // chunk):
            at = pl.ds(pl.multiple_of(piece * part + i * chunk, chunk), chunk)
            x = wide[unit % 2, d, at, :]
            y = narrow[unit % 2, d, at, :].astype(F32)
            put(i * chunk, chunk, ((x + y) * inverse).astype(BF16))

    def issue(unit, first, last, scale=None):
        def one(t, _):
            d, piece, slot, fresh = item(unit, t)
            if unit == 0:
                @pl.when(jnp.logical_not(fresh))
                def _():
                    data(unit, d, piece, slot).wait_send()
            else:
                data(unit, d, piece, slot).wait_send()

            def put(at, size, value):
                send[slot, at:at + size, :] = value

            scaled(unit, d, piece, put, scale)
            data(unit, d, piece, slot).start()
            return 0

        lax.fori_loop(first, last, one, 0)

    def own(unit):
        kind, j = unit // each, unit % each

        def one(piece, _):
            def put(at, size, value):
                readies[kind][j, me, pl.ds(pl.multiple_of(piece * part + at, size), size), :] = value

            scaled(unit, me, piece, put)
            return 0

        lax.fori_loop(0, parts, one, 0)

    rows_of = rows // owners

    def block_of(r):
        return pl.ds(pl.multiple_of(r * rows, rows), rows)

    def share_of(r, o):
        return pl.ds(pl.multiple_of(r * rows + o * rows_of, rows_of), rows_of)

    def r1(k):
        return remote(padded, pieces.at[owner], r1_send.at[k], r1_recv.at[k], owner=(owner + k) % owners)

    def r2(k):
        at = router.at[block_of(me)]
        return remote(at, at, r2_send.at[k], r2_recv.at[k], rows=base + pair(k))

    def r3():
        at = router.at[share_of(me, owner)]
        return remote(at, at, r3_send, r3_recv, rows=mirror)

    def r4(k):
        at = router.at[share_of(mirror, owner)]
        return remote(at, at, r4_send.at[k], r4_recv.at[k], owner=(owner + k) % owners)

    def r5(k):
        at = router.at[block_of(mirror)]
        return remote(at, at, r5_send.at[k], r5_recv.at[k], rows=base + pair(k))

    def router_owners():
        for copy in routing:
            copy.wait()
        columns, lanes = weight.shape[0], padded.shape[1]
        lane = lax.broadcasted_iota(jnp.int32, (columns, lanes), 1)
        row = lax.broadcasted_iota(jnp.int32, (columns, lanes), 0)
        place = (lane == row + owner * columns).astype(F32).astype(BF16)
        mine = (weight[...] * gain[...]).astype(BF16)
        padded[...] = lax.dot_general(mine, place, (((0,), (0,)), ((), ())),
                                      preferred_element_type=F32).astype(BF16)
        pieces[owner] = padded[...]
        for k in range(1, owners):
            r1(k).start()

    def router_rows():
        for k in range(1, owners):
            r1(k).wait()
        total = pieces[0].astype(F32)
        for o in range(1, owners):
            total = total + pieces[o].astype(F32)
        router[block_of(me), :] = total.astype(BF16)
        r3().start()
        for k in range(1, half):
            r2(k).start()

    def router_across():
        r3().wait()
        for k in range(1, owners):
            r4(k).start()

    def router_far():
        for k in range(1, owners):
            r4(k).wait()
        for k in range(1, half):
            r5(k).start()

    maxima(0)
    pl.semaphore_wait(barrier, n - 1 + owners - 1)
    for k in range(1, half):
        to_spot(0, k).start()
    for k in range(1, n):
        to_direct(k).start()
    start(1)
    across(0)
    now = min(FAR_DEEP, parts)
    first = first_scale()
    issue(0, 0, now, first)
    spread(0)
    issue(0, now, parts, first)
    known(0)
    stages = [router_owners, router_rows, router_across, router_far]
    steps = (maxima, across, spread)
    for unit in range(units):
        more = unit + 1 < units
        at = parts if unit == 0 else 0
        marks = [at + (items - at) * mark // 28 for mark in (2, 9, 16)]
        for mark, step in zip(marks, steps):
            issue(unit, at, mark)
            at = mark
            if more:
                step(unit + 1)
        issue(unit, at, items)
        own(unit)
        start(unit + 2)
        if more:
            known(unit + 1)
        if stages:
            stages.pop(0)()
    for stage in stages:
        stage()
    for k in range(1, half):
        r2(k).wait()
        r5(k).wait()
    for slot in range(deep):
        data(0, mirror, 0, slot).wait_send()
    for kind in range(2):
        def ended(k, _, kind=kind):
            d = (me + k) % n
            at = readies[kind].at[:, d]
            remote(at, at, send_sem.at[0], recv_sem.at[kind, d], rows=d).wait_recv()
            return 0

        lax.fori_loop(1, n, ended, 0)


def store(count, *refs):
    sources, results, sem = refs[:count], refs[count:2 * count], refs[2 * count]
    copies = []
    for source, result in zip(sources, results):
        whole = len(source.shape) < 4
        for at in range(1 if whole else source.shape[0] * SPLIT):
            if not whole:
                size = source.shape[1] // SPLIT
                index = (at // SPLIT, pl.ds(at % SPLIT * size, size))
            pieces = (source, result) if whole else (source.at[index], result.at[index])
            copies.append(pltpu.make_async_copy(*pieces, sem.at[len(copies)]))
    for copy in copies:
        copy.start()
    for copy in copies:
        copy.wait()


def stored(arrays):
    count = len(arrays)
    copies = sum(x.shape[0] * SPLIT if x.ndim == 4 else 1 for x in arrays)
    return pl.pallas_call(
        functools.partial(store, count),
        out_shape=tuple(jax.ShapeDtypeStruct(x.shape, x.dtype) for x in arrays),
        in_specs=[pl.BlockSpec(memory_space=pltpu.VMEM)] * count,
        out_specs=(pl.BlockSpec(memory_space=pl.ANY),) * count,
        scratch_shapes=[pltpu.SemaphoreType.DMA((copies,))],
        compiler_params=pltpu.CompilerParams(vmem_limit_bytes=1024 * 1024),
    )(*arrays)


def per_device(n, owners, train_gate, other_gate, train_up, other_up, router_weight, router_gain):
    experts, rows, width = train_gate.shape
    each = experts // n
    units = 2 * each
    half = n // 2
    part = rows // PARTS
    deep = FAR_DEEP + NEAR_DEEP
    columns = router_weight.shape[1]
    blocks = [x.reshape(n, each, rows, width) for x in (train_gate, other_gate, train_up, other_up)]
    hbm, vmem = pl.BlockSpec(memory_space=pl.ANY), pl.BlockSpec(memory_space=pltpu.VMEM)
    dma = pltpu.SemaphoreType.DMA
    scratch = n * rows * width * 12 + deep * part * width * 2 + units * (3 * half + 2) * 2 * width * 4
    results = pl.pallas_call(
        functools.partial(kernel, n, owners, each),
        out_shape=(
            pltpu.VMEM((each, n, rows, width), BF16),
            pltpu.VMEM((each, n, rows, width), BF16),
            pltpu.VMEM((each, width), F32),
            pltpu.VMEM((each, width), F32),
            pltpu.VMEM((n * rows, owners * columns), BF16),
        ),
        in_specs=[hbm] * 4 + [pl.BlockSpec(memory_space=pltpu.HBM)] * 2,
        out_specs=(vmem,) * 5,
        scratch_shapes=[
            pltpu.VMEM((2, n, rows, width), F32),
            pltpu.VMEM((2, n, rows, width), BF16),
            pltpu.VMEM((deep, part, width), BF16),
            pltpu.VMEM((units, half, 2, width), F32),
            pltpu.VMEM((units, half, 2, width), F32),
            pltpu.VMEM((units, 2, width), F32),
            pltpu.VMEM((units, 2, width), F32),
            pltpu.VMEM((units, half, 2, width), F32),
            pltpu.VMEM((n, 1, width), F32),
            pltpu.VMEM((n, 1, width), F32),
            pltpu.VMEM((columns, rows), F32),
            pltpu.VMEM((1, rows), F32),
            pltpu.VMEM((rows, owners * columns), BF16),
            pltpu.VMEM((owners, rows, owners * columns), BF16),
            dma((2, half, 2)), dma((deep,)), dma((2, n)),
            dma((n,)), dma((n,)), dma((2,)),
            dma((half,)), dma((half,)), dma((2,)), dma((2,)), dma((half,)), dma((half,)),
            dma((owners,)), dma((owners,)), dma((half,)), dma((half,)), dma(()), dma(()),
            dma((owners,)), dma((owners,)), dma((half,)), dma((half,)),
        ],
        compiler_params=pltpu.CompilerParams(
            collective_id=0, has_side_effects=True, vmem_limit_bytes=scratch + 4 * 1024 * 1024
        ),
    )(*blocks, router_weight.T, router_gain.reshape(1, rows))
    ready_gate, ready_up, scale_gate, scale_up, router = stored(results)
    ready_gate, ready_up = (x.reshape(each, n * rows, width) for x in (ready_gate, ready_up))
    return (ready_gate, ready_up, scale_gate, scale_up, router)


def solution(mesh):
    n, owners = mesh.shape["rows"], mesh.shape["owner"]
    in_specs = (
        P("owner", "rows", None),
        P("owner", "rows", None),
        P("owner", "rows", None),
        P("owner", "rows", None),
        P("rows", "owner"),
        P("rows"),
    )
    out_specs = (
        P(("owner", "rows"), None, None),
        P(("owner", "rows"), None, None),
        P(("owner", "rows"), None),
        P(("owner", "rows"), None),
        P(),
    )
    return jax.shard_map(
        functools.partial(per_device, n, owners), mesh=mesh, in_specs=in_specs,
        out_specs=out_specs, check_vma=False,
    )
```

time: 609 us -> 564 us (0.926)
  Pallas kernels: 605 us -> 562 us
    pallas_call x1, Pallas kernels: 597 us -> 553 us  [per_device(): pl.pallas_call(functools.partial(kernel, n, owners, each), out_shape=(plt...]
where the time goes in v2:
time: 564 us
  Pallas kernels  562 us (100%)
    pallas_call x1, Pallas kernels, per_device(): pl.pallas_call(functools.partial(kernel, n, owners, each), out_shape=(plt...  553 us

profile of v2, /device:TPU:11, one launch (start us, length us, event | category | flops | bytes accessed | tf_op | source)
XLA Modules:
  0.0 564.0 jit_solution(579780692656138532)
XLA Ops:
  0.6 0.0 copy-start
  0.6 0.7 copy-done
  1.4 0.0 copy-start.1
  1.4 0.7 copy-done.1
  2.1 553.3 %shard_map.101 = (bf16[4,8,256,768]{3,2,1,0:T(8,128)(2,1)S(1)}, bf16[4,8,256,768]{3,2,1,0:T(8,128)(2,1)S(1)}, f32[4,768]{1,0:T(4,128)S(1)}, f32[4,768]{1,0:T(4,128)S(1)}, bf16[2048,128]{1,0:T(8,128)(2,1)S(1)}) custom-call(f32[8,4,256,768]{3,2,1,0:T(8,128)} %bitcast.10, bf16[8,4,256,768]{3,2,1,0:T(8,128)(2,1)} %bitcast.12, f32[8,4,256,768]{3,2,1,0:T(8,128)} %bitcast.11, ...), custom_call_target="tpu_custom_call" | custom-call | tf_op jit(solution)/shard_map/pallas_call | solution.py:392
  555.4 8.7 %shard_map.102 = (bf16[4,8,256,768]{3,2,1,0:T(8,128)(2,1)}, bf16[4,8,256,768]{3,2,1,0:T(8,128)(2,1)}, f32[4,768]{1,0:T(4,128)}, f32[4,768]{1,0:T(4,128)}, bf16[2048,128]{1,0:T(8,128)(2,1)}) custom-call(bf16[4,8,256,768]{3,2,1,0:T(8,128)(2,1)S(1)} %get-tuple-element.15.refs_0_, bf16[4,8,256,768]{3,2,1,0:T(8,128)(2,1)S(1)} %get-tuple-element.16.refs_1_, ...), custom_call_target="tpu_custom_call" | custom-call | tf_op jit(solution)/shard_map/pallas_call | solution.py:370
Async XLA Ops:
  0.6 0.8 copy-start
  1.4 0.7 copy-start.1

commit v3 on v2

--- a/solution.py
+++ b/solution.py
@@ -9,7 +9,7 @@
 
 F32, BF16 = jnp.float32, jnp.bfloat16
 CHUNK = 32
-PARTS, FAR_DEEP, NEAR_DEEP, SPLIT = 4, 3, 4, 2
+PARTS, FAR_DEEP, NEAR_DEEP, SPLIT, COMMON = 4, 3, 4, 2, 6
 
 
 def flipped(me, k, n):
@@ -21,10 +21,10 @@
 
 
 def kernel(n, owners, each, train_gate, other_gate, train_up, other_up, router_weight, router_gain,
-           ready_gate, ready_up, scale_gate, scale_up, router,
+           ready_gate, ready_up, scale_gate, scale_up, router, rest,
            wide, narrow, send, maxes, gathered, halves, mirrored, full, solo, direct,
            weight, gain, padded, pieces,
-           load_sem, send_sem, recv_sem, ds_sem, dr_sem, router_sem,
+           load_sem, send_sem, recv_sem, gate_sem, ds_sem, dr_sem, router_sem,
            as_sem, ar_sem, bs_sem, br_sem, cs_sem, cr_sem,
            r1_send, r1_recv, r2_send, r2_recv, r3_send, r3_recv, r4_send, r4_recv, r5_send, r5_recv):
     me, owner = lax.axis_index("rows"), lax.axis_index("owner")
@@ -165,12 +165,23 @@
         return jnp.where(d % 2 == 0, two[0:1], two[1:2])
 
     far_items, near_items = half * parts, (half - 2) * parts
-    items = far_items + near_items + parts
+    late = far_items // 2
     side = me % 2
+    quarter = me // (half // 2)
+    inner = jnp.logical_or(quarter == 1, quarter == 2)
+
+    def far_count(unit):
+        return far_items if unit < units - 2 else far_items - late
+
+    def far_base(unit):
+        return sum(far_count(u) for u in range(unit))
+
+    def item_count(unit):
+        return far_count(unit) + near_items + parts
 
     def item(unit, t):
         lead = parts if unit == 0 else 0
-        mixed = far_items - lead + near_items
+        mixed = far_count(unit) - lead + near_items
         after = jnp.maximum(t - lead, 0)
         phase = side * (2 * mixed // 3)
         near_at = (after * near_items + phase) // mixed
@@ -182,7 +193,7 @@
         at = jnp.where(is_far, far_at, near_at)
         near_k = jnp.where(beside, 1, 2 + at // parts)
         d = flipped(me, jnp.where(is_far, half + at // parts, near_k), n)
-        slot = jnp.where(is_far, (unit * far_items + far_at) % FAR_DEEP,
+        slot = jnp.where(is_far, (far_base(unit) + far_at) % FAR_DEEP,
                          FAR_DEEP + (unit * (near_items + parts) + near_at) % NEAR_DEEP)
         fresh = at < jnp.where(is_far, FAR_DEEP, NEAR_DEEP)
         return d, at % parts, slot, fresh
@@ -222,6 +233,38 @@
             return 0
 
         lax.fori_loop(first, last, one, 0)
+
+    def late_item(unit, t):
+        far_at = far_items - late + t
+        d = flipped(me, half + far_at // parts, n)
+        return d, far_at % parts, (far_base(units) + t) % FAR_DEEP
+
+    def issue_late(unit, first, last):
+        def one(t, _):
+            d, piece, slot = late_item(unit, t)
+            slot = slot if unit == units - 2 else (slot + late) % FAR_DEEP
+            data(unit, d, piece, slot).wait_send()
+
+            def put(at, size, value):
+                send[slot, at:at + size, :] = value
+
+            scaled(unit, d, piece, put)
+            data(unit, d, piece, slot).start()
+            return 0
+
+        lax.fori_loop(first, last, one, 0)
+
+    def leave(unit):
+        def one(t, _):
+            d, piece, _ = late_item(unit, t)
+
+            def put(at, size, value):
+                rest[d % (half // 2), pl.ds(pl.multiple_of(piece * part + at, size), size), :] = value
+
+            scaled(unit, d, piece, put)
+            return 0
+
+        lax.fori_loop(0, late, one, 0)
 
     def own(unit):
         kind, j = unit // each, unit % each
@@ -317,6 +360,7 @@
     for unit in range(units):
         more = unit + 1 < units
         at = parts if unit == 0 else 0
+        items = item_count(unit)
         marks = [at + (items - at) * mark // 28 for mark in (2, 9, 16)]
         for mark, step in zip(marks, steps):
             issue(unit, at, mark)
@@ -332,49 +376,180 @@
             stages.pop(0)()
     for stage in stages:
         stage()
+    def sent(slot):
+        data(0, mirror, 0, slot).wait_send()
+
+    common = late * COMMON // 8
+    issue_late(units - 2, 0, common)
+
+    @pl.when(inner)
+    def _():
+        issue_late(units - 2, common, late)
+        for t in range(late - FAR_DEEP, late - 1):
+            sent((far_base(units) + t) % FAR_DEEP)
+        pl.semaphore_signal(gate_sem, inc=1, device_id={"rows": flipped(me, half // 2, n)},
+                            device_id_type=pl.DeviceIdType.MESH)
+        leave(units - 1)
+        sent((far_base(units) + late - 1) % FAR_DEEP)
+
+    @pl.when(jnp.logical_not(inner))
+    def _():
+        pl.semaphore_wait(gate_sem, 1)
+        issue_late(units - 2, common, late)
+        issue_late(units - 1, 0, late)
+        for slot in range(FAR_DEEP):
+            sent(slot)
+
     for k in range(1, half):
         r2(k).wait()
         r5(k).wait()
-    for slot in range(deep):
-        data(0, mirror, 0, slot).wait_send()
-    for kind in range(2):
-        def ended(k, _, kind=kind):
-            d = (me + k) % n
-            at = readies[kind].at[:, d]
-            remote(at, at, send_sem.at[0], recv_sem.at[kind, d], rows=d).wait_recv()
+    for slot in range(FAR_DEEP, deep):
+        sent(slot)
+
+    def landed(kind, d, count):
+        at = readies[kind].at[pl.ds(0, count), d]
+        remote(at, at, send_sem.at[0], recv_sem.at[kind, d], rows=d).wait_recv()
+
+    def all_of(kind):
+        def one(k, _):
+            landed(kind, flipped(me, k, n), each)
             return 0
-
-        lax.fori_loop(1, n, ended, 0)
-
-
-def store(count, *refs):
-    sources, results, sem = refs[:count], refs[count:2 * count], refs[2 * count]
+        return one
+
+    lax.fori_loop(1, n, all_of(0), 0)
+    lax.fori_loop(1, n - half // 2, all_of(1), 0)
+
+    @pl.when(jnp.logical_not(inner))
+    def _():
+        lax.fori_loop(n - half // 2, n, all_of(1), 0)
+
+    if each > 1:
+        @pl.when(inner)
+        def _():
+            def one(k, _):
+                landed(1, flipped(me, k, n), each - 1)
+                return 0
+
+            lax.fori_loop(n - half // 2, n, one, 0)
+
+
+def place(n):
+    me = lax.axis_index("rows")
+    group = n // 4
+    quarter = me // group
+    return me, group, quarter, jnp.logical_or(quarter == 1, quarter == 2)
+
+
+def store(n, *refs):
+    count = (len(refs) - 2) // 2
+    sources, results, token, sem = refs[:count], refs[count:2 * count], refs[2 * count], refs[2 * count + 1]
+    token[...] = jnp.zeros_like(token)
+    _, group, quarter, inner = place(n)
     copies = []
-    for source, result in zip(sources, results):
-        whole = len(source.shape) < 4
-        for at in range(1 if whole else source.shape[0] * SPLIT):
-            if not whole:
-                size = source.shape[1] // SPLIT
-                index = (at // SPLIT, pl.ds(at % SPLIT * size, size))
-            pieces = (source, result) if whole else (source.at[index], result.at[index])
-            copies.append(pltpu.make_async_copy(*pieces, sem.at[len(copies)]))
-    for copy in copies:
-        copy.start()
-    for copy in copies:
-        copy.wait()
-
-
-def stored(arrays):
+
+    def copy(i, index=None):
+        pieces = (sources[i], results[i]) if index is None else (sources[i].at[index], results[i].at[index])
+        made = pltpu.make_async_copy(*pieces, sem.at[len(copies)])
+        copies.append(made)
+        return made
+
+    each = sources[0].shape[0]
+    size = n // SPLIT
+    whole = [copy(i) for i in range(2, count)]
+    for i in range(2):
+        for j in range(each if i == 0 else each - 1):
+            whole += [copy(i, (j, pl.ds(at * size, size))) for at in range(SPLIT)]
+    last = [copy(1, (each - 1, pl.ds(c * group, group))) for c in range(4)]
+    for made in whole:
+        made.start()
+
+    def guarded(act):
+        for c, made in enumerate(last):
+            @pl.when(jnp.logical_not(jnp.logical_and(inner, quarter == 3 - c)))
+            def _(made=made):
+                act(made)
+
+    guarded(lambda made: made.start())
+    for made in whole:
+        made.wait()
+    guarded(lambda made: made.wait())
+
+
+def stored(n, arrays):
     count = len(arrays)
-    copies = sum(x.shape[0] * SPLIT if x.ndim == 4 else 1 for x in arrays)
+    copies = count - 2 + (2 * arrays[0].shape[0] - 1) * SPLIT + 4
     return pl.pallas_call(
-        functools.partial(store, count),
-        out_shape=tuple(jax.ShapeDtypeStruct(x.shape, x.dtype) for x in arrays),
+        functools.partial(store, n),
+        out_shape=tuple(jax.ShapeDtypeStruct(x.shape, x.dtype) for x in arrays) + (pltpu.VMEM((8, 128), F32),),
         in_specs=[pl.BlockSpec(memory_space=pltpu.VMEM)] * count,
-        out_specs=(pl.BlockSpec(memory_space=pl.ANY),) * count,
+        out_specs=(pl.BlockSpec(memory_space=pl.ANY),) * count + (pl.BlockSpec(memory_space=pltpu.VMEM),),
         scratch_shapes=[pltpu.SemaphoreType.DMA((copies,))],
         compiler_params=pltpu.CompilerParams(vmem_limit_bytes=1024 * 1024),
     )(*arrays)
+
+
+def swap(n, rest, _, landing, send_sem, recv_sem):
+    me, group, quarter, inner = place(n)
+    base = (3 - quarter) * group
+
+    @pl.when(inner)
+    def _():
+        barrier = pltpu.get_barrier_semaphore()
+        for i in range(group):
+            pl.semaphore_signal(barrier, inc=1, device_id={"rows": base + i},
+                                device_id_type=pl.DeviceIdType.MESH)
+        pl.semaphore_wait(barrier, group)
+        mine = me % group
+
+        def copy(k):
+            i = (mine + k) % group
+            return pltpu.make_async_remote_copy(
+                src_ref=rest.at[i], dst_ref=landing.at[mine], send_sem=send_sem.at[k],
+                recv_sem=recv_sem.at[k], device_id={"rows": base + i},
+                device_id_type=pl.DeviceIdType.MESH)
+
+        for k in range(group):
+            copy(k).start()
+        for k in range(group):
+            copy(k).wait()
+
+
+def swapped(n, rest, after):
+    dma = pltpu.SemaphoreType.DMA
+    group = rest.shape[0]
+    return pl.pallas_call(
+        functools.partial(swap, n),
+        out_shape=pltpu.VMEM(rest.shape, BF16),
+        in_specs=[pl.BlockSpec(memory_space=pltpu.VMEM)] * 2,
+        out_specs=pl.BlockSpec(memory_space=pltpu.VMEM),
+        scratch_shapes=[dma((group,)), dma((group,))],
+        compiler_params=pltpu.CompilerParams(
+            collective_id=1, has_side_effects=True, vmem_limit_bytes=1024 * 1024),
+    )(rest, after)
+
+
+def add(n, ready, landing, result, sem):
+    _, group, quarter, inner = place(n)
+
+    @pl.when(inner)
+    def _():
+        at = pl.ds(pl.multiple_of((3 - quarter) * group, group), group)
+        copy = pltpu.make_async_copy(landing, result.at[result.shape[0] - 1, at], sem)
+        copy.start()
+        copy.wait()
+
+
+def added(n, ready, landing):
+    hbm = pl.BlockSpec(memory_space=pl.ANY)
+    return pl.pallas_call(
+        functools.partial(add, n),
+        out_shape=jax.ShapeDtypeStruct(ready.shape, ready.dtype),
+        in_specs=[hbm, pl.BlockSpec(memory_space=pltpu.VMEM)],
+        out_specs=hbm,
+        scratch_shapes=[pltpu.SemaphoreType.DMA(())],
+        input_output_aliases={0: 0},
+        compiler_params=pltpu.CompilerParams(vmem_limit_bytes=1024 * 1024),
+    )(ready, landing)
 
 
 def per_device(n, owners, train_gate, other_gate, train_up, other_up, router_weight, router_gain):
@@ -397,9 +572,10 @@
             pltpu.VMEM((each, width), F32),
             pltpu.VMEM((each, width), F32),
             pltpu.VMEM((n * rows, owners * columns), BF16),
+            pltpu.VMEM((n // 4, rows, width), BF16),
         ),
         in_specs=[hbm] * 4 + [pl.BlockSpec(memory_space=pltpu.HBM)] * 2,
-        out_specs=(vmem,) * 5,
+        out_specs=(vmem,) * 6,
         scratch_shapes=[
             pltpu.VMEM((2, n, rows, width), F32),
             pltpu.VMEM((2, n, rows, width), BF16),
@@ -415,7 +591,7 @@
             pltpu.VMEM((1, rows), F32),
             pltpu.VMEM((rows, owners * columns), BF16),
             pltpu.VMEM((owners, rows, owners * columns), BF16),
-            dma((2, half, 2)), dma((deep,)), dma((2, n)),
+            dma((2, half, 2)), dma((deep,)), dma((2, n)), pltpu.SemaphoreType.REGULAR,
             dma((n,)), dma((n,)), dma((2,)),
             dma((half,)), dma((half,)), dma((2,)), dma((2,)), dma((half,)), dma((half,)),
             dma((owners,)), dma((owners,)), dma((half,)), dma((half,)), dma(()), dma(()),
@@ -425,7 +601,9 @@
             collective_id=0, has_side_effects=True, vmem_limit_bytes=scratch + 4 * 1024 * 1024
         ),
     )(*blocks, router_weight.T, router_gain.reshape(1, rows))
-    ready_gate, ready_up, scale_gate, scale_up, router = stored(results)
+    ready_gate, ready_up, scale_gate, scale_up, router, token = stored(n, results[:5])
+    landing = swapped(n, results[5], token)
+    ready_up = added(n, ready_up, landing)
     ready_gate, ready_up = (x.reshape(each, n * rows, width) for x in (ready_gate, ready_up))
     return (ready_gate, ready_up, scale_gate, scale_up, router)
 

time: 564 us -> 557 us (0.988)
  Pallas kernels: 562 us -> 555 us
    pallas_call x1, Pallas kernels: 553 us -> 526 us  [per_device(): pl.pallas_call(functools.partial(kernel, n, owners, each), out_shape=(plt...]
    pallas_call x1 -> x3, Pallas kernels: 8.67 us -> 28.8 us  [the longest x1 19.5 us: swapped(): pl.pallas_call(functools.partial(swap, n), out_shape=pltpu.VMEM(rest.shap...]
where the time goes in v3:
time: 557 us
  Pallas kernels  555 us (100%)
    pallas_call x1, Pallas kernels, per_device(): pl.pallas_call(functools.partial(kernel, n, owners, each), out_shape=(plt...  526 us
    pallas_call x1, Pallas kernels, swapped(): pl.pallas_call(functools.partial(swap, n), out_shape=pltpu.VMEM(rest.shap...  19.5 us

profile of v3, /device:TPU:11, one launch (start us, length us, event | category | flops | bytes accessed | tf_op | source)
XLA Modules:
  0.0 556.9 jit_solution(17782557584920147362)
XLA Ops:
  0.6 0.0 copy-start
  0.6 0.7 copy-done
  1.4 0.0 copy-start.1
  1.4 0.7 copy-done.1
  2.1 526.0 %shard_map.101 = (bf16[4,8,256,768]{3,2,1,0:T(8,128)(2,1)S(1)}, bf16[4,8,256,768]{3,2,1,0:T(8,128)(2,1)S(1)}, f32[4,768]{1,0:T(4,128)S(1)}, f32[4,768]{1,0:T(4,1...) custom-call(f32[8,4,256,768]{3,2,1,0:T(8,128)} %bitcast.10, bf16[8,4,256,768]{3,2,1,0:T(8,128)(2,1)} %bitcast.12, ...), custom_call_target="tpu_custom_call" | custom-call | tf_op jit(solution)/shard_map/pallas_call | solution.py:567
  528.1 8.5 %shard_map.102 = (bf16[4,8,256,768]{3,2,1,0:T(8,128)(2,1)}, bf16[4,8,256,768]{3,2,1,0:T(8,128)(2,1)}, f32[4,768]{1,0:T(4,128)}, f32[4,768]{1,0:T(4,128)}, bf16[2...) custom-call(bf16[4,8,256,768]{3,2,1,0:T(8,128)(2,1)S(1)} %get-tuple-element.17.refs_0_, ...), custom_call_target="tpu_custom_call" | custom-call | tf_op jit(solution)/shard_map/pallas_call | solution.py:481
  536.5 19.5 %shard_map.103.landing = bf16[2,256,768]{2,1,0:T(8,128)(2,1)S(1)} custom-call(bf16[2,256,768]{2,1,0:T(8,128)(2,1)S(1)} %get-tuple-element.24.rest, f32[8,128]{1,0:T(8,128)S(1)} %get-tuple-element.25._), custom_call_target="tpu_custom_call" | custom-call | tf_op jit(solution)/shard_map/pallas_call | solution.py:520
  556.0 0.9 shard_map.104
Async XLA Ops:
  0.6 0.8 copy-start
  1.4 0.7 copy-start.1

commit v4 on v3

--- a/solution.py
+++ b/solution.py
@@ -8,6 +8,7 @@
 from jax.sharding import PartitionSpec as P
 
 F32, BF16 = jnp.float32, jnp.bfloat16
+VMEM_BYTES = 67_043_328
 CHUNK = 32
 PARTS, FAR_DEEP, NEAR_DEEP, SPLIT, COMMON = 4, 3, 4, 2, 6
 
@@ -387,14 +388,15 @@
         issue_late(units - 2, common, late)
         for t in range(late - FAR_DEEP, late - 1):
             sent((far_base(units) + t) % FAR_DEEP)
-        pl.semaphore_signal(gate_sem, inc=1, device_id={"rows": flipped(me, half // 2, n)},
-                            device_id_type=pl.DeviceIdType.MESH)
+        for k in range(half // 2, half):
+            pl.semaphore_signal(gate_sem, inc=1, device_id={"rows": flipped(me, k, n)},
+                                device_id_type=pl.DeviceIdType.MESH)
         leave(units - 1)
         sent((far_base(units) + late - 1) % FAR_DEEP)
 
     @pl.when(jnp.logical_not(inner))
     def _():
-        pl.semaphore_wait(gate_sem, 1)
+        pl.semaphore_wait(gate_sem, half // 2)
         issue_late(units - 2, common, late)
         issue_late(units - 1, 0, late)
         for slot in range(FAR_DEEP):
@@ -563,7 +565,7 @@
     blocks = [x.reshape(n, each, rows, width) for x in (train_gate, other_gate, train_up, other_up)]
     hbm, vmem = pl.BlockSpec(memory_space=pl.ANY), pl.BlockSpec(memory_space=pltpu.VMEM)
     dma = pltpu.SemaphoreType.DMA
-    scratch = n * rows * width * 12 + deep * part * width * 2 + units * (3 * half + 2) * 2 * width * 4
+    held = 2 * n * rows * (2 * each * width + owners * columns) + 8 * each * width + n // 4 * rows * width * 2
     results = pl.pallas_call(
         functools.partial(kernel, n, owners, each),
         out_shape=(
@@ -598,7 +600,7 @@
             dma((owners,)), dma((owners,)), dma((half,)), dma((half,)),
         ],
         compiler_params=pltpu.CompilerParams(
-            collective_id=0, has_side_effects=True, vmem_limit_bytes=scratch + 4 * 1024 * 1024
+            collective_id=0, has_side_effects=True, vmem_limit_bytes=VMEM_BYTES - held - 8192
         ),
     )(*blocks, router_weight.T, router_gain.reshape(1, rows))
     ready_gate, ready_up, scale_gate, scale_up, router, token = stored(n, results[:5])

time: 557 us -> 555 us (level)
    pallas_call x1, Pallas kernels: 526 us -> 515 us  [per_device(): pl.pallas_call(functools.partial(kernel, n, owners, each), out_shape=(plt...]
    pallas_call x1, Pallas kernels: 19.5 us -> 29.6 us  [swapped(): pl.pallas_call(functools.partial(swap, n), out_shape=pltpu.VMEM(rest.shap...]
where the time goes in v4:
time: 555 us
  Pallas kernels  555 us (100%)
    pallas_call x1, Pallas kernels, per_device(): pl.pallas_call(functools.partial(kernel, n, owners, each), out_shape=(plt...  515 us
    pallas_call x1, Pallas kernels, swapped(): pl.pallas_call(functools.partial(swap, n), out_shape=pltpu.VMEM(rest.shap...  29.6 us

profile of v4, /device:TPU:11, one launch (start us, length us, event | category | flops | bytes accessed | tf_op | source)
XLA Modules:
  0.0 555.2 jit_solution(14689127696129272766)
XLA Ops:
  0.6 515.5 %shard_map.101 = (bf16[4,8,256,768]{3,2,1,0:T(8,128)(2,1)S(1)}, bf16[4,8,256,768]{3,2,1,0:T(8,128)(2,1)S(1)}, f32[4,768]{1,0:T(4,128)S(1)}, f32[4,768]{1,0:T(4,1...) custom-call(f32[8,4,256,768]{3,2,1,0:T(8,128)} %bitcast.8, bf16[8,4,256,768]{3,2,1,0:T(8,128)(2,1)} %bitcast.10, ...), custom_call_target="tpu_custom_call" | custom-call | tf_op jit(solution)/shard_map/pallas_call | solution.py:569
  516.1 8.5 %shard_map.102 = (bf16[4,8,256,768]{3,2,1,0:T(8,128)(2,1)}, bf16[4,8,256,768]{3,2,1,0:T(8,128)(2,1)}, f32[4,768]{1,0:T(4,128)}, f32[4,768]{1,0:T(4,128)}, bf16[2...) custom-call(bf16[4,8,256,768]{3,2,1,0:T(8,128)(2,1)S(1)} %get-tuple-element.17.refs_0_, ...), custom_call_target="tpu_custom_call" | custom-call | tf_op jit(solution)/shard_map/pallas_call | solution.py:483
  524.6 29.6 %shard_map.103.landing = bf16[2,256,768]{2,1,0:T(8,128)(2,1)S(1)} custom-call(bf16[2,256,768]{2,1,0:T(8,128)(2,1)S(1)} %get-tuple-element.24.rest, f32[8,128]{1,0:T(8,128)S(1)} %get-tuple-element.25._), custom_call_target="tpu_custom_call" | custom-call | tf_op jit(solution)/shard_map/pallas_call | solution.py:522
  554.3 0.9 shard_map.104
